TPU v7x, 256 devices: a whole 4x4x8 slice. The times are simulated.
256 devices in a mesh: bank: 64 (over z, y, core), zero: 4 (over x).
Axes of the slice: x: 4, y: 4, z: 8, core: 2. Of those that a mesh axis runs over, the one named last changes fastest.
Arguments:
- train_down: float32 [128, 768, 2048], P('bank', None, 'zero'), may hold values from -0.3125 to 0.3125
- other_down: float32 [128, 768, 2048], P('bank', None, 'zero'), may hold values from -0.21875 to 0.21875
- router_weight: float32 [2048, 128], P('zero', 'bank'), may hold values from -0.125 to 0.125
- router_gain: float32 [2048], P('zero'), may hold values from 0.25 to 1.75
Outputs:
- ready_down: bfloat16 [128, 768, 2048], P('bank')
- scale_down: float32 [128, 768], P('bank')
- serve_router: bfloat16 [2048, 128], replicated
- latest_down: float32 [128, 768, 2048], P('bank', None, 'zero')
All inputs are finite; a program needn't handle non-finite values. Where the computation divides by a largest or mean magnitude, that divisor is 1e-20 or more.
Results may differ from a plain program's by a relative error of at most 0.001.
Values may be sent and summed in bfloat16 or wider, within the bound.
A program may use at most 128 MiB of HBM per device.

v0:
```python
import jax
import jax.numpy as jnp
from jax import lax
from jax.sharding import Mesh
from jax.sharding import PartitionSpec as P

D_MODEL = 2048
BANK = ("bank_0", "bank_1", "bank_2")


def copy_for_each(x, axis):
    devices = lax.axis_size(axis)
    return lax.all_to_all(jnp.broadcast_to(x[None], (devices, *x.shape)), axis, 0, 0, tiled=True)


def of_everyone(x, axis):
    return copy_for_each(x, axis).sum(axis=0)


def in_order(blocks, dim):
    blocks = jnp.moveaxis(blocks, 0, dim)
    shape = blocks.shape
    return blocks.reshape(*shape[:dim], shape[dim] * shape[dim + 1], *shape[dim + 2 :])


def all_blocks(x, axes, turns):
    blocks = x
    for k in turns:
        blocks = lax.all_gather(blocks, axes[k])
    done = turns[::-1]
    back = [done.index(k) for k in range(len(axes))]
    blocks = blocks.transpose(*back, *range(len(axes), blocks.ndim))
    return blocks.reshape(-1, *x.shape)


def gather_axes(x, axes, turns, dim):
    return in_order(all_blocks(x, axes, turns), dim)


def shards(train_down, other_down, router_weight, router_gain):
    latest_down = 0.5 * other_down + 0.5 * train_down
    total_down = of_everyone(jnp.sum(jnp.abs(latest_down), axis=2), "zero")
    scale_down = total_down / D_MODEL
    narrow_down = (latest_down / jnp.expand_dims(scale_down, 2)).astype(jnp.bfloat16)
    ready_down = lax.all_gather(narrow_down, "zero", axis=2, tiled=True)
    part_router = (router_weight * router_gain[:, None]).astype(jnp.bfloat16)
    row_router = lax.all_gather(part_router, "zero", axis=0, tiled=True)
    serve_router = gather_axes(row_router, BANK, (1, 0, 2), 1)
    return (ready_down, scale_down, serve_router, latest_down)


def solution(mesh):
    split = Mesh(
        mesh.devices.reshape(8, 4, 2, mesh.shape["zero"]), ("bank_0", "bank_1", "bank_2", "zero")
    )
    placed = (P(BANK, None, "zero"), P(BANK, None, "zero"), P("zero", BANK), P("zero"))
    return jax.shard_map(
        shards,
        mesh=split,
        in_specs=placed,
        out_specs=(P(BANK, None, None), P(BANK, None), P(), P(BANK, None, "zero")),
        check_vma=False,
    )
```

profile of v0, /device:TPU:8, one launch (start us, length us, event | category | flops | bytes accessed | tf_op | source)
XLA Modules:
  0.0 104.4 jit_solution(9432049307572382526)
XLA Ops:
  7.2 0.0 all-gather.5.cloned.1.call-start
  7.2 3.3 %abs_reduce_fusion = (f32[2,768]{1,0:T(2,128)S(1)}, f32[2,768,512]{2,1,0:T(8,128)S(1)}) fusion(f32[2,768,512]{2,1,0:T(8,128)} %param.5, f32[2,768,512]{2,1,0:T(8,128)} %param.4), kind=kLoop, calls=%fused_computation.1 | loop fusion | flops 3144192 | bytes 9443328 | tf_op jit(solution)/shard_map/reduce_sum | solution.py:42
  10.6 0.0 copy-start
  10.6 9.5 %all_to_all.5 = f32[4,2,768]{2,1,0:T(2,128)S(1)} all-to-all(f32[4,2,768]{2,1,0:T(2,128)S(1)} %broadcast_in_dim.2), channel_id=1, replica_groups=mesh['bank_0'=8,'bank_1'=4,'bank_2'=2,'zero'=4] {'zero'}, dimensions={0} | all-to-all | bytes 49152 | tf_op jit(solution)/shard_map/all_to_all | solution.py:13
  20.1 0.0 copy-start.1
  20.1 0.0 copy-start.2
  20.1 0.0 copy-start.3
  20.2 1.4 %divide_convert_fusion = bf16[2,768,512]{2,1,0:T(8,128)(2,1)} fusion(f32[2,768,512]{2,1,0:T(8,128)S(1)} %get-tuple-element.33, f32[2,768]{1,0:T(2,128)S(1)} %broadcast_multiply_fusion), kind=kLoop, calls=%fused_computation | loop fusion | flops 1572864 | bytes 4724736 | tf_op jit(solution)/shard_map/convert_element_type | solution.py:44
  21.6 0.0 all-gather.5.cloned.1.call-update
  21.6 0.0 copy-done
  21.6 0.0 copy-done.1
  21.6 0.0 copy-done.2
  21.6 0.0 copy-done.3
  21.7 10.4 %all_gather.25 = bf16[2048,2]{0,1:T(2,128)(2,1)S(1)} all-gather(bf16[512,2]{0,1:T(2,128)(2,1)S(1)} %multiply_convert_fusion), channel_id=1, replica_groups=mesh['bank_0'=8,'bank_1'=4,'bank_2'=2,'zero'=4] {'zero'}, dimensions={0}, use_global_device_ids=true | all-gather | bytes 10240 | tf_op jit(solution)/shard_map/all_gather | solution.py:47
  32.1 12.1 %all-gather = bf16[8192,2]{0,1:T(2,128)(2,1)S(1)} all-gather(bf16[2048,2]{0,1:T(2,128)(2,1)S(1)} %all_gather.25), channel_id=2, replica_groups=mesh['bank_0'=8,'bank_1'=4,'bank_2'=2,'zero'=4] {'bank_1'}, dimensions={0}, use_global_device_ids=true | all-gather | bytes 40960 | tf_op jit(solution)/shard_map/all_gather | solution.py:29
  44.2 28.5 %all-gather.1 = bf16[32,2048,2]{1,2,0:T(2,128)(2,1)S(1)} all-gather(bf16[4,2048,2]{1,2,0:T(2,128)(2,1)S(1)} %bitcast.15), channel_id=3, replica_groups=mesh['bank_0'=8,'bank_1'=4,'bank_2'=2,'zero'=4] {'bank_0'}, dimensions={0}, use_global_device_ids=true | all-gather | bytes 294912 | tf_op jit(solution)/shard_map/all_gather | solution.py:29
  72.7 0.1 copy.22
  72.9 2.2 %all-gather.2 = bf16[16,4,2048,2]{2,1,3,0:T(4,128)(2,1)S(1)} all-gather(bf16[8,4,2048,2]{2,1,3,0:T(4,128)(2,1)S(1)} %copy.22), channel_id=4, replica_groups=mesh['bank_0'=8,'bank_1'=4,'bank_2'=2,'zero'=4] {'bank_2'}, dimensions={0}, use_global_device_ids=true | all-gather | bytes 786432 | tf_op jit(solution)/shard_map/all_gather | solution.py:29
  75.0 0.3 copy.28
  75.3 0.5 copy.24
  75.9 0.2 reshape.20
  76.1 1.0 copy.25
  77.1 13.9 %all-gather.5.cloned.1.call-done = bf16[2,768,2048]{2,1,0:T(8,128)(2,1)} async-done(((bf16[2,768,512]{2,1,0:T(8,128)(2,1)}), bf16[2,768,2048]{2,1,0:T(8,128)(2,1)}) %all-gather.5.cloned.1.call-update) | async-done | bytes 6291472 | tf_op jit(solution)/shard_map/all_gather | solution.py:45
  90.9 6.6 %copy.30 = bf16[2,768,2048]{2,1,0:T(8,128)(2,1)} copy(bf16[2,768,2048]{2,1,0:T(8,128)(2,1)} %all-gather.5.cloned.1.call-done) | data formatting | bytes 12582912
  (4 shorter events, 0.0 us)
Async XLA Ops:
  7.2 83.8 %all-gather.5.cloned.1.call-start = ((), (), s32[]{:S(2)}) async-start(), calls=%async_computation.1 | async-start | bytes 7864320 | tf_op jit(solution)/shard_map/all_gather | solution.py:45
  10.6 11.1 %copy-start = (f32[2,768,512]{2,1,0:T(8,128)}, f32[2,768,512]{2,1,0:T(8,128)S(1)}, u32[]{:S(2)}) copy-start(f32[2,768,512]{2,1,0:T(8,128)S(1)} %get-tuple-element.33) | copy-start | bytes 9437188
  20.1 1.5 %copy-start.1 = (f32[2,768]{1,0:T(2,128)}, f32[2,768]{1,0:T(2,128)S(1)}, u32[]{:S(2)}) copy-start(f32[2,768]{1,0:T(2,128)S(1)} %broadcast_multiply_fusion) | copy-start | bytes 18436
  20.1 1.5 %copy-start.2 = (f32[512,2]{0,1:T(2,128)S(1)}, f32[512,2]{0,1:T(2,128)}, u32[]{:S(2)}) copy-start(f32[512,2]{0,1:T(2,128)} %param.6) | copy-start | bytes 12292
  20.1 1.5 %copy-start.3 = (f32[512]{0:T(512)S(1)}, f32[512]{0:T(512)}, u32[]{:S(2)}) copy-start(f32[512]{0:T(512)} %param.7) | copy-start | bytes 6148
Sparse Core Ops, SparseCore 0:
  21.7 69.1 all-gather.4
where the time goes:
time: 105 us; the launch traced here: 104 us
  blocking collectives  62.7 us (60%)
  between operations  14.1 us (13%)
  waiting for transfers between devices  13.9 us (13%)
  local copies, waits for them, and re-layouts  8.81 us (8%)
  other arithmetic  4.81 us (5%)
    all_gather x3, blocking collectives, all_blocks(): blocks = lax.all_gather(blocks, axes[k])  42.8 us
    all_gather x1, waiting for transfers between devices, shards(): ready_down = lax.all_gather(narrow_down, 'zero', axis=2, tiled=True)  13.9 us
    all_gather x1, blocking collectives, shards(): row_router = lax.all_gather(part_router, 'zero', axis=0, tiled=True)  10.4 us
    all_to_all x1, blocking collectives, copy_for_each(): lax.all_to_all(jnp.broadcast_to(x[None], (devices, *x.shape)), axis, 0, 0...  9.5 us
    unnamed x10, local copies, waits for them, and re-layouts  7.64 us
    reduce_sum x1, other arithmetic, shards(): total_down = of_everyone(jnp.sum(jnp.abs(latest_down), axis=2), 'zero')  3.34 us
  transfers between devices with their start and end apart: 1, of which 1 were waited for; matrix products, arithmetic and copies ran while one was open for 2% of the time, Pallas kernels for 0%

commit v1 on v0

v1 whole, which is shorter than its diff:
```python
import functools

import jax
import jax.numpy as jnp
from jax import lax
from jax.experimental import pallas as pl
from jax.experimental.pallas import tpu as pltpu
from jax.sharding import PartitionSpec as P

MESH = pl.DeviceIdType.MESH
D_MODEL = 2048
ROWS = 1536
PART = 512
BLOCK = 128
BLOCKS = ROWS // BLOCK
CHUNK = 256
CHUNKS = ROWS // CHUNK
HALF = CHUNKS // 2
NZ, NY, NC, NX = 8, 4, 2, 4


def kernel(
    train, other, weight, gain,
    ready, scale, router, latest,
    train_v, other_v, weight_v, gain_v, sums, rows_r, wide_r,
    in_sem, small_sem, sum_s, sum_r, rx_s, rx_r, ry_s, ry_r, rz_s, rz_r, rc_s, rc_r,
    own_s, own_r, far_s, far_r,
):
    me = lax.axis_index("zero")
    bank = lax.axis_index("bank")
    z, y, core = bank // (NY * NC), lax.rem(bank // NC, NY), lax.rem(bank, NC)
    right, left, opposite = (lax.rem(me + k, NX) for k in (1, 3, 2))
    bank_of = lambda z, y, core: (z * NY + y) * NC + core
    z_up, z_down = lax.rem(z + 1, NZ), lax.rem(z + NZ - 1, NZ)
    y_up, y_down = lax.rem(y + 1, NY), lax.rem(y + NY - 1, NY)
    at_y_up, at_y_down = {"bank": bank_of(z, y_up, core)}, {"bank": bank_of(z, y_down, core)}
    at_z_up, at_z_down = {"bank": bank_of(z_up, y, core)}, {"bank": bank_of(z_down, y, core)}
    at_core = {"bank": bank_of(z, y, 1 - core)}
    at_x = [{"zero": right}, {"zero": left}, {"zero": opposite}]

    barrier = pltpu.get_barrier_semaphore()
    for peer in (*at_x, at_y_up, at_y_down, at_z_up, at_z_down, at_core):
        pl.semaphore_signal(barrier, inc=1, device_id=peer, device_id_type=MESH)

    def read(c):
        rows = pl.ds(c * CHUNK, CHUNK)
        return [
            pltpu.make_async_copy(train.at[rows], train_v.at[rows], in_sem.at[0, c]),
            pltpu.make_async_copy(other.at[rows], other_v.at[rows], in_sem.at[1, c]),
        ]

    small = [
        pltpu.make_async_copy(weight, weight_v, small_sem.at[0]),
        pltpu.make_async_copy(gain, gain_v, small_sem.at[1]),
    ]
    reads = [read(c) for c in range(CHUNKS)]
    for copy in (*reads[0], *small, *(r for c in range(1, CHUNKS) for r in reads[c])):
        copy.start()

    def send(src, dst, s, r, to):
        copy = pltpu.make_async_remote_copy(
            src_ref=src, dst_ref=dst, send_sem=s, recv_sem=r, device_id=to, device_id_type=MESH
        )
        copy.start()
        return copy

    def average(c):
        for copy in reads[c]:
            copy.wait()
        for b in range(c * CHUNK // BLOCK, (c + 1) * CHUNK // BLOCK):
            rows = pl.ds(b * BLOCK, BLOCK)
            mixed = 0.5 * other_v[rows, :] + 0.5 * train_v[rows, :]
            latest[rows, :] = mixed
            size = jnp.abs(mixed)
            lanes = sum(size[:, k * 128 : (k + 1) * 128] for k in range(1, PART // 128)) + size[:, :128]
            sums[me, b] = jnp.sum(lanes.T, axis=0, keepdims=True)

    def send_sums(first, last, group):
        blocks = pl.ds(first, last - first)
        return [
            send(sums.at[me, blocks], sums.at[me, blocks], sum_s.at[group, k], sum_r.at[group, k], at_x[k])
            for k in range(3)
        ]

    def narrow(c):
        for b in range(c * CHUNK // BLOCK, (c + 1) * CHUNK // BLOCK):
            rows = pl.ds(b * BLOCK, BLOCK)
            mean = ((sums[0, b] + sums[1, b]) + (sums[2, b] + sums[3, b])) / D_MODEL
            per = BLOCKS // 2
            scale[b // per : b // per + 1, (b % per) * BLOCK : (b % per + 1) * BLOCK] = mean
            factor = jnp.broadcast_to(1.0 / mean, (BLOCK, BLOCK)).T
            for k in range(PART // 128):
                columns = pl.ds(pl.multiple_of(me * PART + k * 128, 128), 128)
                ready[rows, columns] = (latest[rows, k * 128 : (k + 1) * 128] * factor).astype(jnp.bfloat16)

    def block_of(c, x):
        return ready.at[pl.ds(c * CHUNK, CHUNK), pl.ds(pl.multiple_of(x * PART, PART), PART)]

    average(0)
    for copy in small:
        copy.wait()
    rows_r[z, y, core, me] = (weight_v[...] * gain_v[...]).astype(jnp.bfloat16)
    pl.semaphore_wait(barrier, 8)

    first_sums = send_sums(0, CHUNK // BLOCK, 0)
    mine = rows_r.at[z, y, core, me]
    sent = [send(mine, mine, rx_s.at[k], rx_r.at[k], at_x[k]) for k in range(3)]
    for c in range(1, CHUNKS):
        average(c)
    other_sums = send_sums(CHUNK // BLOCK, BLOCKS, 1)

    own = []
    for c in range(CHUNKS):
        if c == 0:
            for copy in first_sums:
                copy.wait_recv()
        if c == 1:
            for copy in other_sums:
                copy.wait_recv()
        narrow(c)
        block = block_of(c, me)
        own.append([send(block, block, own_s.at[k, c], own_r.at[k, c], at_x[k]) for k in range(2)])

    for copy in sent:
        copy.wait_recv()
    line = rows_r.at[z, y, core]
    y_sent = [
        send(line, line, ry_s.at[0], ry_r.at[0], at_y_up),
        send(line, line, ry_s.at[1], ry_r.at[1], at_y_down),
    ]
    for copy in y_sent:
        copy.wait_recv()
    line = rows_r.at[z, y_down, core]
    y_sent.append(send(line, line, ry_s.at[2], ry_r.at[2], at_y_up))
    y_sent[2].wait_recv()
    sent += y_sent
    for step in range(NZ // 2):
        plane = rows_r.at[lax.rem(z + NZ - step, NZ), :, core]
        up = [send(plane, plane, rz_s.at[0, step], rz_r.at[0, step], at_z_up)]
        if step < NZ // 2 - 1:
            plane = rows_r.at[lax.rem(z + step, NZ), :, core]
            up.append(send(plane, plane, rz_s.at[1, step], rz_r.at[1, step], at_z_down))
        for copy in up:
            copy.wait_recv()
        sent += up
    side = rows_r.at[:, :, core]
    sent.append(send(side, side, rc_s, rc_r, at_core))
    sent[-1].wait_recv()

    def widen(i, carry):
        for j in range(NC):
            for x in range(NX):
                piece = rows_r[i // NY, lax.rem(i, NY), j, x].astype(jnp.float32)
                wide_r[i, 2 * j : 2 * j + 2, x * PART : (x + 1) * PART] = piece
        return carry

    lax.fori_loop(0, NZ * NY, widen, 0)

    def turn(i, carry):
        columns = pl.ds(pl.multiple_of(i * 128, 128), 128)
        tile = wide_r[:, :, columns].reshape(128, 128)
        router[columns, :] = tile.T.astype(jnp.bfloat16)
        return carry

    lax.fori_loop(0, D_MODEL // 128, turn, 0)

    far = []
    for c in range(CHUNKS):
        k = 0 if c < HALF else 1
        own[c][k].wait_recv()
        block = block_of(c, left if k == 0 else right)
        far.append(send(block, block, far_s.at[c], far_r.at[c], at_x[k]))
    for c in range(CHUNKS):
        own[c][1 if c < HALF else 0].wait_recv()
    for copy in far:
        copy.wait_recv()
    for copy in (*first_sums, *other_sums, *sent, *(k for pair in own for k in pair), *far):
        copy.wait_send()


def write(ready, scale, router, latest, ready_out, scale_out, router_out, latest_out, sem):
    pieces = [(ready, ready_out, k, ROWS // 6) for k in range(6)]
    pieces += [(latest, latest_out, k, ROWS // 3) for k in range(3)]
    pieces += [(router, router_out, 0, D_MODEL), (scale, scale_out, 0, 2)]
    copies = [
        pltpu.make_async_copy(src.at[pl.ds(k * n, n)], dst.at[pl.ds(k * n, n)], sem.at[i])
        for i, (src, dst, k, n) in enumerate(pieces)
    ]
    for copy in copies:
        copy.start()
    for copy in copies:
        copy.wait()


def shards(train_down, other_down, router_weight, router_gain):
    f32, bf16 = jnp.float32, jnp.bfloat16
    dma = pltpu.SemaphoreType.DMA
    shapes = (((ROWS, D_MODEL), bf16), ((2, ROWS // 2), f32), ((D_MODEL, 128), bf16), ((ROWS, PART), f32))
    given = (
        train_down.reshape(ROWS, PART),
        other_down.reshape(ROWS, PART),
        router_weight.T,
        router_gain.reshape(1, PART),
    )
    made = pl.pallas_call(
        kernel,
        out_shape=tuple(pltpu.VMEM(*k) for k in shapes),
        in_specs=[pl.BlockSpec(memory_space=pltpu.HBM)] * 4,
        out_specs=[pl.BlockSpec(memory_space=pltpu.VMEM)] * 4,
        scratch_shapes=[
            pltpu.VMEM((ROWS, PART), f32),
            pltpu.VMEM((ROWS, PART), f32),
            pltpu.VMEM((2, PART), f32),
            pltpu.VMEM((1, PART), f32),
            pltpu.VMEM((NX, BLOCKS, 1, BLOCK), f32),
            pltpu.VMEM((NZ, NY, NC, NX, 2, PART), bf16),
            pltpu.VMEM((NZ * NY, 2 * NC, D_MODEL), f32),
            dma((2, CHUNKS)), dma((2,)),
            dma((2, 3)), dma((2, 3)),
            dma((3,)), dma((3,)),
            dma((3,)), dma((3,)),
            dma((2, NZ // 2)), dma((2, NZ // 2)),
            dma, dma,
            dma((2, CHUNKS)), dma((2, CHUNKS)),
            dma((CHUNKS,)), dma((CHUNKS,)),
        ],
        compiler_params=pltpu.CompilerParams(
            collective_id=0, has_side_effects=True, vmem_limit_bytes=16 * 2**20
        ),
    )(*(pltpu.with_memory_space_constraint(k, pltpu.HBM) for k in given))
    ready, scale, router, latest = pl.pallas_call(
        write,
        out_shape=tuple(pltpu.HBM(*k) for k in shapes),
        in_specs=[pl.BlockSpec(memory_space=pltpu.VMEM)] * 4,
        out_specs=[pl.BlockSpec(memory_space=pltpu.HBM)] * 4,
        scratch_shapes=[dma((11,))],
        compiler_params=pltpu.CompilerParams(vmem_limit_bytes=2**20),
    )(*made)
    return ready.reshape(2, ROWS // 2, D_MODEL), scale, router, latest.reshape(2, ROWS // 2, PART)


def solution(mesh):
    return jax.shard_map(
        shards,
        mesh=mesh,
        in_specs=(P("bank", None, "zero"), P("bank", None, "zero"), P("zero", "bank"), P("zero")),
        out_specs=(P("bank", None, None), P("bank", None), P(), P("bank", None, "zero")),
        check_vma=False,
    )
```

time: 105 us -> 67.6 us (0.64)
  Pallas kernels: 0 us -> 66.8 us
  blocking collectives: 62.7 us -> 0 us
  waiting for transfers between devices: 13.9 us -> 0 us
  between operations: 14.1 us -> 0.64 us
  local copies, waits for them, and re-layouts: 8.81 us -> 0 us
  other arithmetic: 4.81 us -> 0 us
    pallas_call x0 -> x2, Pallas kernels: none -> 66.8 us  [the longest x1 63 us: shards(): pl.pallas_call(kernel, out_shape=tuple((pltpu.VMEM(*k) for k in shapes)),...]
    all_gather x4 -> x0, blocking collectives: 53.2 us -> none  [the longest x3 42.8 us: all_blocks(): blocks = lax.all_gather(blocks, axes[k])]
    all_gather x1 -> x0, waiting for transfers between devices: 13.9 us -> none  [shards(): ready_down = lax.all_gather(narrow_down, 'zero', axis=2, tiled=True)]
    all_to_all x1 -> x0, blocking collectives: 9.5 us -> none  [copy_for_each(): lax.all_to_all(jnp.broadcast_to(x[None], (devices, *x.shape)), axis, 0, 0...]
    unnamed x10 -> x0, local copies, waits for them, and re-layouts: 7.64 us -> none
    reduce_sum x2 -> x0, other arithmetic: 3.36 us -> none  [the longest x1 3.34 us: shards(): total_down = of_everyone(jnp.sum(jnp.abs(latest_down), axis=2), 'zero')]
    convert_element_type x2 -> x0, other arithmetic: 1.44 us -> none  [the longest x1 1.43 us: shards(): (latest_down / jnp.expand_dims(scale_down, 2)).astype(jnp.bfloat16)]
  transfers between devices with their start and end apart: 1 -> 0, of which waited for: 1 -> 0; matrix products, arithmetic and copies ran while one was open for 2% -> 0% of each run, Pallas kernels for 0% -> 0%
where the time goes in v1:
time: 67.6 us; the launch traced here: 67.5 us
  Pallas kernels  66.8 us (99%)
    pallas_call x1, Pallas kernels, shards(): pl.pallas_call(kernel, out_shape=tuple((pltpu.VMEM(*k) for k in shapes)),...  63 us
    pallas_call x1, Pallas kernels, shards(): pl.pallas_call(write, out_shape=tuple((pltpu.HBM(*k) for k in shapes)), i...  3.85 us

profile of v1, /device:TPU:8, one launch (start us, length us, event | category | flops | bytes accessed | tf_op | source)
XLA Modules:
  0.0 67.5 jit_solution(4672514204313819002)
XLA Ops:
  0.6 63.0 %shard_map.75 = (bf16[1536,2048]{1,0:T(8,128)(2,1)S(1)}, f32[2,768]{1,0:T(2,128)S(1)}, bf16[2048,128]{1,0:T(8,128)(2,1)S(1)}, f32[1536,512]{1,0:T(8,128)S(1)}) custom-call(f32[1536,512]{1,0:T(8,128)} %bitcast.6, f32[1536,512]{1,0:T(8,128)} %bitcast.7, f32[2,512]{1,0:T(2,128)} %bitcast.8, f32[1,512]{1,0:T(1,128)} %bitcast.9), custom_call_target="tpu_custom_call" | custom-call | tf_op jit(solution)/shard_map/pallas_call | solution.py:205
  63.6 3.9 %shard_map.76 = (bf16[1536,2048]{1,0:T(8,128)(2,1)}, f32[2,768]{1,0:T(2,128)}, bf16[2048,128]{1,0:T(8,128)(2,1)}, f32[1536,512]{1,0:T(8,128)}) custom-call(bf16[1536,2048]{1,0:T(8,128)(2,1)S(1)} %get-tuple-element.12.ready, f32[2,768]{1,0:T(2,128)S(1)} %get-tuple-element.13.scale, bf16[2048,128]{1,0:T(8,128)(2,1)S(1)} %get-tuple-element.14.router, ...), custom_call_target="tpu_custom_call" | custom-call | tf_op jit(solution)/shard_map/pallas_call | solution.py:231

commit v2 on v1

--- a/solution.py
+++ b/solution.py
@@ -13,18 +13,23 @@
 PART = 512
 BLOCK = 128
 BLOCKS = ROWS // BLOCK
-CHUNK = 256
-CHUNKS = ROWS // CHUNK
-HALF = CHUNKS // 2
+FILL = 128
+FILLS = 4
+EARLY = 4
+EDGES = (FILL, 256, 512, 768, 1024, 1280, 1536)
+CHUNKS = len(EDGES) - 1
+FAR = (0, 256, 512, 768, 1024, 1280, 1536)
+HALF = 3
+READS = (0, 128, 512, 1024, 1536)
 NZ, NY, NC, NX = 8, 4, 2, 4
 
 
 def kernel(
     train, other, weight, gain,
     ready, scale, router, latest,
-    train_v, other_v, weight_v, gain_v, sums, rows_r, wide_r,
-    in_sem, small_sem, sum_s, sum_r, rx_s, rx_r, ry_s, ry_r, rz_s, rz_r, rc_s, rc_r,
-    own_s, own_r, far_s, far_r,
+    train_v, other_v, weight_v, gain_v, sums, fill, rows_r, wide_r,
+    z_ready, in_sem, small_sem, sum_s, sum_r, rx_s, rx_r, ry_s, ry_r, rz_s, rz_r, rc_s, rc_r,
+    fill_s, fill_r, own_s, own_r, far_s, far_r,
 ):
     me = lax.axis_index("zero")
     bank = lax.axis_index("bank")
@@ -38,12 +43,18 @@
     at_core = {"bank": bank_of(z, y, 1 - core)}
     at_x = [{"zero": right}, {"zero": left}, {"zero": opposite}]
 
+    even = lax.rem(z, 2) == 0
     barrier = pltpu.get_barrier_semaphore()
-    for peer in (*at_x, at_y_up, at_y_down, at_z_up, at_z_down, at_core):
+    for peer in (*at_x, at_y_up, at_y_down, at_core):
         pl.semaphore_signal(barrier, inc=1, device_id=peer, device_id_type=MESH)
 
+    @pl.when(even)
+    def _():
+        for peer in (at_z_up, at_z_down):
+            pl.semaphore_signal(barrier, inc=1, device_id=peer, device_id_type=MESH)
+
     def read(c):
-        rows = pl.ds(c * CHUNK, CHUNK)
+        rows = pl.ds(READS[c], READS[c + 1] - READS[c])
         return [
             pltpu.make_async_copy(train.at[rows], train_v.at[rows], in_sem.at[0, c]),
             pltpu.make_async_copy(other.at[rows], other_v.at[rows], in_sem.at[1, c]),
@@ -53,8 +64,8 @@
         pltpu.make_async_copy(weight, weight_v, small_sem.at[0]),
         pltpu.make_async_copy(gain, gain_v, small_sem.at[1]),
     ]
-    reads = [read(c) for c in range(CHUNKS)]
-    for copy in (*reads[0], *small, *(r for c in range(1, CHUNKS) for r in reads[c])):
+    reads = [read(c) for c in range(len(READS) - 1)]
+    for copy in (*reads[0], *reads[1], *small, *reads[2], *reads[3]):
         copy.start()
 
     def send(src, dst, s, r, to):
@@ -67,7 +78,7 @@
     def average(c):
         for copy in reads[c]:
             copy.wait()
-        for b in range(c * CHUNK // BLOCK, (c + 1) * CHUNK // BLOCK):
+        for b in range(READS[c] // BLOCK, READS[c + 1] // BLOCK):
             rows = pl.ds(b * BLOCK, BLOCK)
             mixed = 0.5 * other_v[rows, :] + 0.5 * train_v[rows, :]
             latest[rows, :] = mixed
@@ -79,47 +90,80 @@
         blocks = pl.ds(first, last - first)
         return [
             send(sums.at[me, blocks], sums.at[me, blocks], sum_s.at[group, k], sum_r.at[group, k], at_x[k])
-            for k in range(3)
+            for k in (2, 0, 1)
         ]
 
-    def narrow(c):
-        for b in range(c * CHUNK // BLOCK, (c + 1) * CHUNK // BLOCK):
-            rows = pl.ds(b * BLOCK, BLOCK)
-            mean = ((sums[0, b] + sums[1, b]) + (sums[2, b] + sums[3, b])) / D_MODEL
-            per = BLOCKS // 2
-            scale[b // per : b // per + 1, (b % per) * BLOCK : (b % per + 1) * BLOCK] = mean
-            factor = jnp.broadcast_to(1.0 / mean, (BLOCK, BLOCK)).T
-            for k in range(PART // 128):
-                columns = pl.ds(pl.multiple_of(me * PART + k * 128, 128), 128)
-                ready[rows, columns] = (latest[rows, k * 128 : (k + 1) * 128] * factor).astype(jnp.bfloat16)
-
-    def block_of(c, x):
-        return ready.at[pl.ds(c * CHUNK, CHUNK), pl.ds(pl.multiple_of(x * PART, PART), PART)]
+    def mean(b):
+        return ((sums[0, b] + sums[1, b]) + (sums[2, b] + sums[3, b])) / D_MODEL
+
+    def factor(b):
+        return jnp.broadcast_to(1.0 / mean(b), (BLOCK, BLOCK)).T
+
+    def narrow(b):
+        per = BLOCKS // 2
+        rows = pl.ds(b * BLOCK, BLOCK)
+        scale[b // per : b // per + 1, (b % per) * BLOCK : (b % per + 1) * BLOCK] = mean(b)
+        times = factor(b)
+        for k in range(PART // 128):
+            columns = pl.ds(pl.multiple_of(me * PART + k * 128, 128), 128)
+            ready[rows, columns] = (latest[rows, k * 128 : (k + 1) * 128] * times).astype(jnp.bfloat16)
+
+    def narrow_fill(side, x):
+        times = factor(0)[:FILL]
+        for k in range(PART // 128):
+            columns = pl.ds(pl.multiple_of(x * PART + k * 128, 128), 128)
+            ready[:FILL, columns] = (fill[side, :, k * 128 : (k + 1) * 128] * times).astype(jnp.bfloat16)
+
+    def block_of(first, last, x):
+        return ready.at[pl.ds(first, last - first), pl.ds(pl.multiple_of(x * PART, PART), PART)]
+
+    def send_fill(i):
+        rows = pl.ds(i * (FILL // FILLS), FILL // FILLS)
+        return [
+            send(latest.at[rows], fill.at[1 - k, rows], fill_s.at[k, i], fill_r.at[k, i], at_x[k])
+            for k in range(2)
+        ]
 
     average(0)
     for copy in small:
         copy.wait()
     rows_r[z, y, core, me] = (weight_v[...] * gain_v[...]).astype(jnp.bfloat16)
-    pl.semaphore_wait(barrier, 8)
-
-    first_sums = send_sums(0, CHUNK // BLOCK, 0)
+    pl.semaphore_wait(barrier, 6 + 2 * lax.rem(z, 2))
+
+    @pl.when(jnp.logical_not(even))
+    def _():
+        for peer in (at_z_up, at_z_down):
+            pl.semaphore_signal(z_ready, inc=1, device_id=peer, device_id_type=MESH)
+
+    filled = [send_fill(0)]
+    average(1)
+    first_sums = send_sums(0, EARLY, 0)
     mine = rows_r.at[z, y, core, me]
     sent = [send(mine, mine, rx_s.at[k], rx_r.at[k], at_x[k]) for k in range(3)]
-    for c in range(1, CHUNKS):
-        average(c)
-    other_sums = send_sums(CHUNK // BLOCK, BLOCKS, 1)
+    filled.append(send_fill(1))
+    average(2)
+    average(3)
+    other_sums = send_sums(EARLY, BLOCKS, 1)
+    for i in range(2, FILLS):
+        filled.append(send_fill(i))
 
     own = []
+    for copy in first_sums:
+        copy.wait_recv()
     for c in range(CHUNKS):
-        if c == 0:
-            for copy in first_sums:
-                copy.wait_recv()
-        if c == 1:
+        if EDGES[c] == EARLY * BLOCK:
+            narrow(0)
             for copy in other_sums:
                 copy.wait_recv()
-        narrow(c)
-        block = block_of(c, me)
+        for b in range(EDGES[c] // BLOCK, EDGES[c + 1] // BLOCK):
+            narrow(b)
+        block = block_of(EDGES[c], EDGES[c + 1], me)
         own.append([send(block, block, own_s.at[k, c], own_r.at[k, c], at_x[k]) for k in range(2)])
+    for pair in filled:
+        for copy in pair:
+            copy.wait_recv()
+    narrow_fill(0, right)
+    narrow_fill(1, left)
 
     for copy in sent:
         copy.wait_recv()
@@ -134,6 +178,11 @@
     y_sent.append(send(line, line, ry_s.at[2], ry_r.at[2], at_y_up))
     y_sent[2].wait_recv()
     sent += y_sent
+
+    @pl.when(even)
+    def _():
+        pl.semaphore_wait(z_ready, 2)
+
     for step in range(NZ // 2):
         plane = rows_r.at[lax.rem(z + NZ - step, NZ), :, core]
         up = [send(plane, plane, rz_s.at[0, step], rz_r.at[0, step], at_z_up)]
@@ -165,17 +214,18 @@
     lax.fori_loop(0, D_MODEL // 128, turn, 0)
 
     far = []
-    for c in range(CHUNKS):
+    for c in range(len(FAR) - 1):
         k = 0 if c < HALF else 1
         own[c][k].wait_recv()
-        block = block_of(c, left if k == 0 else right)
+        block = block_of(FAR[c], FAR[c + 1], left if k == 0 else right)
         far.append(send(block, block, far_s.at[c], far_r.at[c], at_x[k]))
     for c in range(CHUNKS):
         own[c][1 if c < HALF else 0].wait_recv()
     for copy in far:
         copy.wait_recv()
-    for copy in (*first_sums, *other_sums, *sent, *(k for pair in own for k in pair), *far):
-        copy.wait_send()
+    for pair in (*filled, *own, first_sums, other_sums, sent, far):
+        for copy in pair:
+            copy.wait_send()
 
 
 def write(ready, scale, router, latest, ready_out, scale_out, router_out, latest_out, sem):
@@ -213,16 +263,19 @@
             pltpu.VMEM((2, PART), f32),
             pltpu.VMEM((1, PART), f32),
             pltpu.VMEM((NX, BLOCKS, 1, BLOCK), f32),
+            pltpu.VMEM((2, FILL, PART), f32),
             pltpu.VMEM((NZ, NY, NC, NX, 2, PART), bf16),
             pltpu.VMEM((NZ * NY, 2 * NC, D_MODEL), f32),
-            dma((2, CHUNKS)), dma((2,)),
+            pltpu.SemaphoreType.REGULAR,
+            dma((2, len(READS) - 1)), dma((2,)),
             dma((2, 3)), dma((2, 3)),
             dma((3,)), dma((3,)),
             dma((3,)), dma((3,)),
             dma((2, NZ // 2)), dma((2, NZ // 2)),
             dma, dma,
+            dma((2, FILLS)), dma((2, FILLS)),
             dma((2, CHUNKS)), dma((2, CHUNKS)),
-            dma((CHUNKS,)), dma((CHUNKS,)),
+            dma((len(FAR) - 1,)), dma((len(FAR) - 1,)),
         ],
         compiler_params=pltpu.CompilerParams(
             collective_id=0, has_side_effects=True, vmem_limit_bytes=16 * 2**20

time: 67.6 us -> 66.6 us (0.985); the launches traced: 67.5 us -> 65.5 us
  Pallas kernels: 66.8 us -> 64.9 us
    pallas_call x1, Pallas kernels: 63 us -> 61 us  [shards(): pl.pallas_call(kernel, out_shape=tuple((pltpu.VMEM(*k) for k in shapes)),...]
where the time goes in v2:
time: 66.6 us; the launch traced here: 65.5 us
  Pallas kernels  64.9 us (97%)
    pallas_call x1, Pallas kernels, shards(): pl.pallas_call(kernel, out_shape=tuple((pltpu.VMEM(*k) for k in shapes)),...  61 us
    pallas_call x1, Pallas kernels, shards(): pl.pallas_call(write, out_shape=tuple((pltpu.HBM(*k) for k in shapes)), i...  3.85 us

profile of v2, /device:TPU:8, one launch (start us, length us, event | category | flops | bytes accessed | tf_op | source)
XLA Modules:
  0.0 65.5 jit_solution(2411304468430549716)
XLA Ops:
  0.6 61.0 %shard_map.75 = (bf16[1536,2048]{1,0:T(8,128)(2,1)S(1)}, f32[2,768]{1,0:T(2,128)S(1)}, bf16[2048,128]{1,0:T(8,128)(2,1)S(1)}, f32[1536,512]{1,0:T(8,128)S(1)}) custom-call(f32[1536,512]{1,0:T(8,128)} %bitcast.6, f32[1536,512]{1,0:T(8,128)} %bitcast.7, f32[2,512]{1,0:T(2,128)} %bitcast.8, f32[1,512]{1,0:T(1,128)} %bitcast.9), custom_call_target="tpu_custom_call" | custom-call | tf_op jit(solution)/shard_map/pallas_call | solution.py:255
  61.7 3.9 %shard_map.76 = (bf16[1536,2048]{1,0:T(8,128)(2,1)}, f32[2,768]{1,0:T(2,128)}, bf16[2048,128]{1,0:T(8,128)(2,1)}, f32[1536,512]{1,0:T(8,128)}) custom-call(bf16[1536,2048]{1,0:T(8,128)(2,1)S(1)} %get-tuple-element.12.ready, f32[2,768]{1,0:T(2,128)S(1)} %get-tuple-element.13.scale, bf16[2048,128]{1,0:T(8,128)(2,1)S(1)} %get-tuple-element.14.router, ...), custom_call_target="tpu_custom_call" | custom-call | tf_op jit(solution)/shard_map/pallas_call | solution.py:284

commit v3 on v2

--- a/solution.py
+++ b/solution.py
@@ -13,14 +13,14 @@
 PART = 512
 BLOCK = 128
 BLOCKS = ROWS // BLOCK
-FILL = 128
-FILLS = 4
-EARLY = 4
-EDGES = (FILL, 256, 512, 768, 1024, 1280, 1536)
+FILL = 64
+FILLS = 1
+READS = (0, 128, 256, 512, 1024, 1536)
+EARLY = 2
+EDGES = (FILL, 128, 256, 512, 768, 1024, 1280, 1536)
 CHUNKS = len(EDGES) - 1
 FAR = (0, 256, 512, 768, 1024, 1280, 1536)
-HALF = 3
-READS = (0, 128, 512, 1024, 1536)
+ORDERS = (0, 1, 2, 3, 4, 5, 6), (0, 1, 4, 5, 6, 2, 3)
 NZ, NY, NC, NX = 8, 4, 2, 4
 
 
@@ -28,7 +28,7 @@
     train, other, weight, gain,
     ready, scale, router, latest,
     train_v, other_v, weight_v, gain_v, sums, fill, rows_r, wide_r,
-    z_ready, in_sem, small_sem, sum_s, sum_r, rx_s, rx_r, ry_s, ry_r, rz_s, rz_r, rc_s, rc_r,
+    line_ready, z_ready, go, in_sem, small_sem, sum_s, sum_r, rx_s, rx_r, ry_s, ry_r, rz_s, rz_r, rc_s, rc_r,
     fill_s, fill_r, own_s, own_r, far_s, far_r,
 ):
     me = lax.axis_index("zero")
@@ -43,15 +43,24 @@
     at_core = {"bank": bank_of(z, y, 1 - core)}
     at_x = [{"zero": right}, {"zero": left}, {"zero": opposite}]
 
+    lead = me == 0
     even = lax.rem(z, 2) == 0
+    near, above = (at_y_up, at_y_down, at_core), (at_z_up, at_z_down)
     barrier = pltpu.get_barrier_semaphore()
-    for peer in (*at_x, at_y_up, at_y_down, at_core):
-        pl.semaphore_signal(barrier, inc=1, device_id=peer, device_id_type=MESH)
-
-    @pl.when(even)
-    def _():
-        for peer in (at_z_up, at_z_down):
-            pl.semaphore_signal(barrier, inc=1, device_id=peer, device_id_type=MESH)
+
+    def tell(peers, semaphore):
+        for peer in peers:
+            pl.semaphore_signal(semaphore, inc=1, device_id=peer, device_id_type=MESH)
+
+    tell(at_x, barrier)
+
+    @pl.when(lead)
+    def _():
+        tell(near, barrier)
+
+    @pl.when(lead & even)
+    def _():
+        tell(above, barrier)
 
     def read(c):
         rows = pl.ds(READS[c], READS[c + 1] - READS[c])
@@ -65,7 +74,7 @@
         pltpu.make_async_copy(gain, gain_v, small_sem.at[1]),
     ]
     reads = [read(c) for c in range(len(READS) - 1)]
-    for copy in (*reads[0], *reads[1], *small, *reads[2], *reads[3]):
+    for copy in (*small, *reads[0], *reads[1]):
         copy.start()
 
     def send(src, dst, s, r, to):
@@ -125,45 +134,88 @@
         ]
 
     average(0)
+    for pair in reads[EARLY:]:
+        for copy in pair:
+            copy.start()
+    average(1)
     for copy in small:
         copy.wait()
     rows_r[z, y, core, me] = (weight_v[...] * gain_v[...]).astype(jnp.bfloat16)
-    pl.semaphore_wait(barrier, 6 + 2 * lax.rem(z, 2))
-
-    @pl.when(jnp.logical_not(even))
-    def _():
-        for peer in (at_z_up, at_z_down):
-            pl.semaphore_signal(z_ready, inc=1, device_id=peer, device_id_type=MESH)
-
-    filled = [send_fill(0)]
-    average(1)
-    first_sums = send_sums(0, EARLY, 0)
+    pl.semaphore_wait(barrier, jnp.where(lead, 6 + 2 * lax.rem(z, 2), 3))
+
+    first_sums = send_sums(0, READS[EARLY] // BLOCK, 0)
     mine = rows_r.at[z, y, core, me]
     sent = [send(mine, mine, rx_s.at[k], rx_r.at[k], at_x[k]) for k in range(3)]
-    filled.append(send_fill(1))
-    average(2)
-    average(3)
-    other_sums = send_sums(EARLY, BLOCKS, 1)
-    for i in range(2, FILLS):
+    filled = [send_fill(0)]
+
+    @pl.when(lead)
+    def _():
+        tell(near, line_ready)
+
+    @pl.when(lead & jnp.logical_not(even))
+    def _():
+        tell(above, line_ready)
+
+    for c in range(EARLY, len(READS) - 1):
+        average(c)
+    other_sums = send_sums(READS[EARLY] // BLOCK, BLOCKS, 1)
+    for i in range(1, FILLS):
         filled.append(send_fill(i))
 
-    own = []
+    own = {}
     for copy in first_sums:
         copy.wait_recv()
-    for c in range(CHUNKS):
-        if EDGES[c] == EARLY * BLOCK:
-            narrow(0)
-            for copy in other_sums:
-                copy.wait_recv()
-        for b in range(EDGES[c] // BLOCK, EDGES[c + 1] // BLOCK):
-            narrow(b)
-        block = block_of(EDGES[c], EDGES[c + 1], me)
-        own.append([send(block, block, own_s.at[k, c], own_r.at[k, c], at_x[k]) for k in range(2)])
+    narrowed, done = READS[EARLY], set()
+    for order in zip(*ORDERS):
+        for k, c in enumerate(order):
+            if EDGES[c + 1] > narrowed == READS[EARLY]:
+                for copy in other_sums:
+                    copy.wait_recv()
+                narrowed = ROWS
+            for b in range(EDGES[c] // BLOCK, EDGES[c + 1] // BLOCK):
+                if b not in done:
+                    done.add(b)
+                    narrow(b)
+            block = block_of(EDGES[c], EDGES[c + 1], me)
+            own[k, c] = send(block, block, own_s.at[k, c], own_r.at[k, c], at_x[k])
     for pair in filled:
         for copy in pair:
             copy.wait_recv()
     narrow_fill(0, right)
     narrow_fill(1, left)
+
+    far, held = [], set(own)
+
+    def take(k, first, last):
+        for c in range(CHUNKS):
+            if (k, c) in held and EDGES[c] < last and EDGES[c + 1] > first:
+                held.remove((k, c))
+                own[k, c].wait_recv()
+
+    def pass_on(*chunks):
+        for c in chunks:
+            k = 0 if FAR[c] < ROWS // 2 else 1
+            take(k, FAR[c], FAR[c + 1])
+            block = block_of(FAR[c], FAR[c + 1], left if k == 0 else right)
+            far.append(send(block, block, far_s.at[c], far_r.at[c], at_x[k]))
+
+    @pl.when(lead & even)
+    def _():
+        pl.semaphore_wait(line_ready, 5)
+        tell(above, z_ready)
+
+    @pl.when(lead & jnp.logical_not(even))
+    def _():
+        pl.semaphore_wait(line_ready, 3)
+        pl.semaphore_wait(z_ready, 2)
+
+    @pl.when(lead)
+    def _():
+        tell(at_x, go)
+
+    @pl.when(jnp.logical_not(lead))
+    def _():
+        pl.semaphore_wait(go, 1)
 
     for copy in sent:
         copy.wait_recv()
@@ -178,10 +230,7 @@
     y_sent.append(send(line, line, ry_s.at[2], ry_r.at[2], at_y_up))
     y_sent[2].wait_recv()
     sent += y_sent
-
-    @pl.when(even)
-    def _():
-        pl.semaphore_wait(z_ready, 2)
+    pass_on(0, 3)
 
     for step in range(NZ // 2):
         plane = rows_r.at[lax.rem(z + NZ - step, NZ), :, core]
@@ -192,6 +241,8 @@
         for copy in up:
             copy.wait_recv()
         sent += up
+        if step % 2 == 1:
+            pass_on(step // 2 + 1, step // 2 + 4)
     side = rows_r.at[:, :, core]
     sent.append(send(side, side, rc_s, rc_r, at_core))
     sent[-1].wait_recv()
@@ -213,17 +264,11 @@
 
     lax.fori_loop(0, D_MODEL // 128, turn, 0)
 
-    far = []
-    for c in range(len(FAR) - 1):
-        k = 0 if c < HALF else 1
-        own[c][k].wait_recv()
-        block = block_of(FAR[c], FAR[c + 1], left if k == 0 else right)
-        far.append(send(block, block, far_s.at[c], far_r.at[c], at_x[k]))
-    for c in range(CHUNKS):
-        own[c][1 if c < HALF else 0].wait_recv()
+    for k in range(2):
+        take(k, 0, ROWS)
     for copy in far:
         copy.wait_recv()
-    for pair in (*filled, *own, first_sums, other_sums, sent, far):
+    for pair in (*filled, own.values(), first_sums, other_sums, sent, far):
         for copy in pair:
             copy.wait_send()
 
@@ -266,7 +311,7 @@
             pltpu.VMEM((2, FILL, PART), f32),
             pltpu.VMEM((NZ, NY, NC, NX, 2, PART), bf16),
             pltpu.VMEM((NZ * NY, 2 * NC, D_MODEL), f32),
-            pltpu.SemaphoreType.REGULAR,
+            *[pltpu.SemaphoreType.REGULAR] * 3,
             dma((2, len(READS) - 1)), dma((2,)),
             dma((2, 3)), dma((2, 3)),
             dma((3,)), dma((3,)),

time: 66.6 us -> 62.9 us (0.944); the launches traced: 65.5 us -> 62.8 us
  Pallas kernels: 64.9 us -> 62.2 us
    pallas_call x1, Pallas kernels: 61 us -> 58.3 us  [shards(): pl.pallas_call(kernel, out_shape=tuple((pltpu.VMEM(*k) for k in shapes)),...]
where the time goes in v3:
time: 62.9 us; the launch traced here: 62.8 us
  Pallas kernels  62.2 us (99%)
  between operations  0.64 us (1%)
    pallas_call x1, Pallas kernels, shards(): pl.pallas_call(kernel, out_shape=tuple((pltpu.VMEM(*k) for k in shapes)),...  58.3 us
    pallas_call x1, Pallas kernels, shards(): pl.pallas_call(write, out_shape=tuple((pltpu.HBM(*k) for k in shapes)), i...  3.85 us

profile of v3, /device:TPU:8, one launch (start us, length us, event | category | flops | bytes accessed | tf_op | source)
XLA Modules:
  0.0 62.8 jit_solution(11060950851854832573)
XLA Ops:
  0.6 58.3 %shard_map.75 = (bf16[1536,2048]{1,0:T(8,128)(2,1)S(1)}, f32[2,768]{1,0:T(2,128)S(1)}, bf16[2048,128]{1,0:T(8,128)(2,1)S(1)}, f32[1536,512]{1,0:T(8,128)S(1)}) custom-call(f32[1536,512]{1,0:T(8,128)} %bitcast.6, f32[1536,512]{1,0:T(8,128)} %bitcast.7, f32[2,512]{1,0:T(2,128)} %bitcast.8, f32[1,512]{1,0:T(1,128)} %bitcast.9), custom_call_target="tpu_custom_call" | custom-call | tf_op jit(solution)/shard_map/pallas_call | solution.py:300
  58.9 3.9 %shard_map.76 = (bf16[1536,2048]{1,0:T(8,128)(2,1)}, f32[2,768]{1,0:T(2,128)}, bf16[2048,128]{1,0:T(8,128)(2,1)}, f32[1536,512]{1,0:T(8,128)}) custom-call(bf16[1536,2048]{1,0:T(8,128)(2,1)S(1)} %get-tuple-element.12.ready, f32[2,768]{1,0:T(2,128)S(1)} %get-tuple-element.13.scale, bf16[2048,128]{1,0:T(8,128)(2,1)S(1)} %get-tuple-element.14.router, ...), custom_call_target="tpu_custom_call" | custom-call | tf_op jit(solution)/shard_map/pallas_call | solution.py:329

commit v4 on v1

v4 whole, which is shorter than its diff:
```python
import jax
import jax.numpy as jnp
from jax import lax
from jax.experimental import pallas as pl
from jax.experimental.pallas import tpu as pltpu
from jax.sharding import PartitionSpec as P

MESH = pl.DeviceIdType.MESH
D_MODEL = 2048
ROWS = 1536
PART = 512
BLOCK = 128
BLOCKS = ROWS // BLOCK
FILL = (48, 64)
READS = (0, 128, 256, 768, 1536)
EARLY = 256
HALF = ROWS // 2
NZ, NY, NC, NX = 8, 4, 2, 4


def kernel(
    train, other, weight, gain,
    ready, scale, router, latest,
    given_v, weight_v, gain_v, sums, fill, rows_r, wide_r,
    clear, in_sem, small_sem, out_sem, sum_r, x_r, y_r, z_r, core_r, first_r, pass_r, last_r,
):
    me = lax.axis_index("zero")
    bank = lax.axis_index("bank")
    z, y, core = bank // (NY * NC), lax.rem(bank // NC, NY), lax.rem(bank, NC)
    right, left, opposite = (lax.rem(me + k, NX) for k in (1, 3, 2))
    bank_of = lambda z, y, core: (z * NY + y) * NC + core
    z_up, z_down = lax.rem(z + 1, NZ), lax.rem(z + NZ - 1, NZ)
    y_up, y_down = lax.rem(y + 1, NY), lax.rem(y + NY - 1, NY)
    at_y_up, at_y_down = {"bank": bank_of(z, y_up, core)}, {"bank": bank_of(z, y_down, core)}
    at_z_up, at_z_down = {"bank": bank_of(z_up, y, core)}, {"bank": bank_of(z_down, y, core)}
    at_core = {"bank": bank_of(z, y, 1 - core)}
    at_x = [{"zero": right}, {"zero": left}, {"zero": opposite}]
    lead = me == 0
    even = lax.rem(z, 2) == 0
    near, above = (at_y_up, at_y_down, at_core), (at_z_up, at_z_down)
    barrier = pltpu.get_barrier_semaphore()

    def tell(peers, semaphore):
        for peer in peers:
            pl.semaphore_signal(semaphore, inc=1, device_id=peer, device_id_type=MESH)

    tell(at_x, barrier)

    @pl.when(lead)
    def _():
        tell(near, barrier)

    @pl.when(lead & even)
    def _():
        tell(above, barrier)

    def start_read(c):
        first, last = READS[c], READS[c + 1]
        for k, source in enumerate((train, other)):
            pltpu.make_async_copy(
                source.at[first:last], given_v.at[k * ROWS + first : k * ROWS + last], in_sem.at[c]
            ).start()

    def wait(size, semaphore):
        pltpu.make_async_copy(size, size, semaphore).wait()

    small = [
        pltpu.make_async_copy(weight, weight_v, small_sem.at[0]),
        pltpu.make_async_copy(gain, gain_v, small_sem.at[1]),
    ]
    for copy in small:
        copy.start()
    start_read(0)
    start_read(1)

    def send(src, dst, r, to):
        pltpu.make_async_remote_copy(
            src_ref=src, dst_ref=dst, send_sem=out_sem, recv_sem=r, device_id=to, device_id_type=MESH
        ).start()

    def average(c):
        wait(given_v.at[: 2 * (READS[c + 1] - READS[c])], in_sem.at[c])
        for b in range(READS[c] // BLOCK, READS[c + 1] // BLOCK):
            first, last = b * BLOCK, (b + 1) * BLOCK
            mixed = 0.5 * given_v[ROWS + first : ROWS + last, :] + 0.5 * given_v[first:last, :]
            latest[first:last, :] = mixed
            size = jnp.abs(mixed)
            lanes = sum(size[:, k * 128 : (k + 1) * 128] for k in range(1, PART // 128)) + size[:, :128]
            sums[me, b] = jnp.sum(lanes.T, axis=0, keepdims=True)

    def sums_of(x, group):
        first, last = ((0, EARLY), (EARLY, ROWS))[group]
        return sums.at[x, first // BLOCK : last // BLOCK]

    def send_sums(group):
        for k in (2, 0, 1):
            send(sums_of(me, group), sums_of(me, group), sum_r.at[group], at_x[k])

    def wait_sums(group):
        wait(sums_of(slice(0, NX - 1), group), sum_r.at[group])

    def mean(b):
        return ((sums[0, b] + sums[1, b]) + (sums[2, b] + sums[3, b])) / D_MODEL

    def factor(b):
        return jnp.broadcast_to(1.0 / mean(b), (BLOCK, BLOCK)).T

    def narrow(first, last):
        for b in range(first // BLOCK, last // BLOCK):
            rows = pl.ds(b * BLOCK, BLOCK)
            per = BLOCKS // 2
            scale[b // per : b // per + 1, (b % per) * BLOCK : (b % per + 1) * BLOCK] = mean(b)
            times = factor(b)
            for k in range(PART // 128):
                columns = pl.ds(pl.multiple_of(me * PART + k * 128, 128), 128)
                ready[rows, columns] = (latest[rows, k * 128 : (k + 1) * 128] * times).astype(jnp.bfloat16)

    def narrow_fill(side, x, rows):
        times = factor(0)[:rows]
        for k in range(PART // 128):
            columns = pl.ds(pl.multiple_of(x * PART + k * 128, 128), 128)
            ready[:rows, columns] = (fill[side, :rows, k * 128 : (k + 1) * 128] * times).astype(jnp.bfloat16)

    def block_of(first, last, x):
        return ready.at[pl.ds(first, last - first), pl.ds(pl.multiple_of(x * PART, PART), PART)]

    def send_block(first, last, x, r, k):
        block = block_of(first, last, x)
        send(block, block, r, at_x[k])

    def by_core(act):
        for i, rows in enumerate(FILL):

            @pl.when(core == i)
            def _():
                act(rows)

    def send_fill(rows):
        for k in range(2):
            send(latest.at[:rows], fill.at[1 - k, :rows], first_r, at_x[k])

    def send_first(rows):
        for k in range(2):
            send_block(rows, BLOCK, me, first_r, k)

    def take_first(rows):
        wait(given_v.at[: BLOCK + rows], first_r)
        narrow_fill(0, right, rows)
        narrow_fill(1, left, rows)

    average(0)
    for c in range(2, len(READS) - 1):
        start_read(c)
    average(1)
    for copy in small:
        copy.wait()
    rows_r[z, y, core, me] = (weight_v[...] * gain_v[...]).astype(jnp.bfloat16)
    pl.semaphore_wait(barrier, jnp.where(lead, 6 + 2 * lax.rem(z, 2), 3))

    send_sums(0)
    by_core(send_fill)
    mine = rows_r.at[z, y, core, me]
    for k in range(3):
        send(mine, mine, x_r, at_x[k])

    @pl.when(lead)
    def _():
        tell(near, clear)

    @pl.when(lead & jnp.logical_not(even))
    def _():
        tell(above, clear)

    for c in range(2, len(READS) - 1):
        average(c)
    send_sums(1)

    wait_sums(0)
    narrow(0, BLOCK)
    by_core(send_first)
    narrow(BLOCK, EARLY)
    send_block(BLOCK, EARLY, me, pass_r.at[0], 0)
    send_block(BLOCK, EARLY, me, last_r, 1)
    wait_sums(1)
    narrow(EARLY, HALF)
    send_block(EARLY, HALF, me, pass_r.at[0], 0)
    narrow(HALF, ROWS)
    send_block(HALF, ROWS, me, pass_r.at[1], 1)
    send_block(HALF, ROWS, me, last_r, 0)
    send_block(EARLY, HALF, me, last_r, 1)
    by_core(take_first)

    @pl.when(lead)
    def _():
        pl.semaphore_wait(clear, 5)
        tell(at_x, clear)

    @pl.when(lead & even)
    def _():
        tell(above, clear)

    @pl.when(jnp.logical_not(lead))
    def _():
        pl.semaphore_wait(clear, 1)

    wait(rows_r.at[z, y, core, : NX - 1], x_r)
    line = rows_r.at[z, y, core]
    send(line, line, y_r.at[0], at_y_up)
    send(line, line, y_r.at[0], at_y_down)
    wait(rows_r.at[z, :2, core], y_r.at[0])
    line = rows_r.at[z, y_down, core]
    send(line, line, y_r.at[1], at_y_up)
    wait(line, y_r.at[1])

    for step in range(NZ // 2):
        plane = rows_r.at[lax.rem(z + NZ - step, NZ), :, core]
        send(plane, plane, z_r.at[step], at_z_up)
        if step < NZ // 2 - 1:
            plane = rows_r.at[lax.rem(z + step, NZ), :, core]
            send(plane, plane, z_r.at[step], at_z_down)
            wait(rows_r.at[:2, :, core], z_r.at[step])
        else:
            wait(plane, z_r.at[step])

    wait(block_of(BLOCK, HALF, left), pass_r.at[0])
    send_block(0, HALF, left, last_r, 0)
    wait(block_of(HALF, ROWS, right), pass_r.at[1])
    send_block(HALF, ROWS, right, last_r, 1)

    side = rows_r.at[:, :, core]
    send(side, side, core_r, at_core)
    wait(side, core_r)

    def widen(i, carry):
        for j in range(NC):
            for x in range(NX):
                piece = rows_r[i // NY, lax.rem(i, NY), j, x].astype(jnp.float32)
                wide_r[i, 2 * j : 2 * j + 2, x * PART : (x + 1) * PART] = piece
        return carry

    lax.fori_loop(0, NZ * NY, widen, 0)

    def turn(i, carry):
        columns = pl.ds(pl.multiple_of(i * 128, 128), 128)
        tile = wide_r[:, :, columns].reshape(128, 128)
        router[columns, :] = tile.T.astype(jnp.bfloat16)
        return carry

    lax.fori_loop(0, D_MODEL // 128, turn, 0)

    wait(given_v.at[: ((ROWS - HALF) + (HALF - BLOCK) + 2 * HALF) // 2], last_r)

    def end(rows):
        blocks = 2 * (ROWS - BLOCK) + 2 * HALF + 2 * (BLOCK + rows)
        sums_and_router = 3 * BLOCKS // 2 + 3 * 2 + 3 * 8 + 7 * 32 + 256
        wait(given_v.at[: (blocks + sums_and_router) // 2], out_sem)

    by_core(end)


def write(ready, scale, router, latest, ready_out, scale_out, router_out, latest_out, sem):
    pairs = (ready, ready_out), (latest, latest_out), (router, router_out), (scale, scale_out)
    copies = [pltpu.make_async_copy(src, dst, sem.at[i]) for i, (src, dst) in enumerate(pairs)]
    for copy in copies:
        copy.start()
    for copy in copies:
        copy.wait()


def shards(train_down, other_down, router_weight, router_gain):
    f32, bf16 = jnp.float32, jnp.bfloat16
    dma = pltpu.SemaphoreType.DMA
    shapes = (((ROWS, D_MODEL), bf16), ((2, ROWS // 2), f32), ((D_MODEL, 128), bf16), ((ROWS, PART), f32))
    given = (
        train_down.reshape(ROWS, PART),
        other_down.reshape(ROWS, PART),
        router_weight.T,
        router_gain.reshape(1, PART),
    )
    made = pl.pallas_call(
        kernel,
        out_shape=tuple(pltpu.VMEM(*k) for k in shapes),
        in_specs=[pl.BlockSpec(memory_space=pltpu.HBM)] * 4,
        out_specs=[pl.BlockSpec(memory_space=pltpu.VMEM)] * 4,
        scratch_shapes=[
            pltpu.VMEM((2 * ROWS, PART), f32),
            pltpu.VMEM((2, PART), f32),
            pltpu.VMEM((1, PART), f32),
            pltpu.VMEM((NX, BLOCKS, 1, BLOCK), f32),
            pltpu.VMEM((2, max(FILL), PART), f32),
            pltpu.VMEM((NZ, NY, NC, NX, 2, PART), bf16),
            pltpu.VMEM((NZ * NY, 2 * NC, D_MODEL), f32),
            pltpu.SemaphoreType.REGULAR,
            dma((len(READS) - 1,)), dma((2,)), dma, dma((2,)), dma, dma((2,)), dma((NZ // 2,)), dma, dma, dma((2,)), dma,
        ],
        compiler_params=pltpu.CompilerParams(
            collective_id=0, has_side_effects=True, vmem_limit_bytes=16 * 2**20
        ),
    )(*(pltpu.with_memory_space_constraint(k, pltpu.HBM) for k in given))
    ready, scale, router, latest = pl.pallas_call(
        write,
        out_shape=tuple(pltpu.HBM(*k) for k in shapes),
        in_specs=[pl.BlockSpec(memory_space=pltpu.VMEM)] * 4,
        out_specs=[pl.BlockSpec(memory_space=pltpu.HBM)] * 4,
        scratch_shapes=[dma((4,))],
        compiler_params=pltpu.CompilerParams(vmem_limit_bytes=2**20),
    )(*made)
    return ready.reshape(2, ROWS // 2, D_MODEL), scale, router, latest.reshape(2, ROWS // 2, PART)


def solution(mesh):
    return jax.shard_map(
        shards,
        mesh=mesh,
        in_specs=(P("bank", None, "zero"), P("bank", None, "zero"), P("zero", "bank"), P("zero")),
        out_specs=(P("bank", None, None), P("bank", None), P(), P("bank", None, "zero")),
        check_vma=False,
    )
```

time: 67.6 us -> 62.1 us (0.919)
  Pallas kernels: 66.8 us -> 61.3 us
    pallas_call x1, Pallas kernels: 63 us -> 57.5 us  [shards(): pl.pallas_call(kernel, out_shape=tuple((pltpu.VMEM(*k) for k in shapes)),...]
where the time goes in v4:
time: 62.1 us; the launch traced here: 62 us
  Pallas kernels  61.3 us (99%)
  between operations  0.64 us (1%)
    pallas_call x1, Pallas kernels, shards(): pl.pallas_call(kernel, out_shape=tuple((pltpu.VMEM(*k) for k in shapes)),...  57.5 us
    pallas_call x1, Pallas kernels, shards(): pl.pallas_call(write, out_shape=tuple((pltpu.HBM(*k) for k in shapes)), i...  3.85 us

profile of v4, /device:TPU:8, one launch (start us, length us, event | category | flops | bytes accessed | tf_op | source)
XLA Modules:
  0.0 62.0 jit_solution(2437994259665129630)
XLA Ops:
  0.6 57.5 %shard_map.75 = (bf16[1536,2048]{1,0:T(8,128)(2,1)S(1)}, f32[2,768]{1,0:T(2,128)S(1)}, bf16[2048,128]{1,0:T(8,128)(2,1)S(1)}, f32[1536,512]{1,0:T(8,128)S(1)}) custom-call(f32[1536,512]{1,0:T(8,128)} %bitcast.6, f32[1536,512]{1,0:T(8,128)} %bitcast.7, f32[2,512]{1,0:T(2,128)} %bitcast.8, f32[1,512]{1,0:T(1,128)} %bitcast.9), custom_call_target="tpu_custom_call" | custom-call | tf_op jit(solution)/shard_map/pallas_call | solution.py:280
  58.1 3.8 %shard_map.76 = (bf16[1536,2048]{1,0:T(8,128)(2,1)}, f32[2,768]{1,0:T(2,128)}, bf16[2048,128]{1,0:T(8,128)(2,1)}, f32[1536,512]{1,0:T(8,128)}) custom-call(bf16[1536,2048]{1,0:T(8,128)(2,1)S(1)} %get-tuple-element.12.ready, f32[2,768]{1,0:T(2,128)S(1)} %get-tuple-element.13.scale, bf16[2048,128]{1,0:T(8,128)(2,1)S(1)} %get-tuple-element.14.router, ...), custom_call_target="tpu_custom_call" | custom-call | tf_op jit(solution)/shard_map/pallas_call | solution.py:300

commit v5 on v4

--- a/solution.py
+++ b/solution.py
@@ -15,6 +15,7 @@
 READS = (0, 128, 256, 768, 1536)
 EARLY = 256
 HALF = ROWS // 2
+SHIFT = 32
 NZ, NY, NC, NX = 8, 4, 2, 4
 
 
@@ -135,6 +136,13 @@
             def _():
                 act(rows)
 
+    def by_edge(x, act):
+        for condition, rows in ((x == 1, HALF + SHIFT), (x == 2, HALF - SHIFT), ((x == 0) | (x == 3), HALF)):
+
+            @pl.when(condition)
+            def _():
+                act(rows)
+
     def send_fill(rows):
         for k in range(2):
             send(latest.at[:rows], fill.at[1 - k, :rows], first_r, at_x[k])
@@ -182,12 +190,15 @@
     send_block(BLOCK, EARLY, me, pass_r.at[0], 0)
     send_block(BLOCK, EARLY, me, last_r, 1)
     wait_sums(1)
-    narrow(EARLY, HALF)
-    send_block(EARLY, HALF, me, pass_r.at[0], 0)
-    narrow(HALF, ROWS)
-    send_block(HALF, ROWS, me, pass_r.at[1], 1)
-    send_block(HALF, ROWS, me, last_r, 0)
-    send_block(EARLY, HALF, me, last_r, 1)
+    narrow(EARLY, ROWS)
+
+    def send_rest(edge):
+        send_block(EARLY, edge, me, pass_r.at[0], 0)
+        send_block(edge, ROWS, me, pass_r.at[1], 1)
+        send_block(edge, ROWS, me, last_r, 0)
+        send_block(EARLY, edge, me, last_r, 1)
+
+    by_edge(me, send_rest)
     by_core(take_first)
 
     @pl.when(lead)
@@ -222,10 +233,16 @@
         else:
             wait(plane, z_r.at[step])
 
-    wait(block_of(BLOCK, HALF, left), pass_r.at[0])
-    send_block(0, HALF, left, last_r, 0)
-    wait(block_of(HALF, ROWS, right), pass_r.at[1])
-    send_block(HALF, ROWS, right, last_r, 1)
+    def pass_right(edge):
+        wait(block_of(BLOCK, edge, left), pass_r.at[0])
+        send_block(0, edge, left, last_r, 0)
+
+    def pass_left(edge):
+        wait(block_of(edge, ROWS, right), pass_r.at[1])
+        send_block(edge, ROWS, right, last_r, 1)
+
+    by_edge(left, pass_right)
+    by_edge(right, pass_left)
 
     side = rows_r.at[:, :, core]
     send(side, side, core_r, at_core)
@@ -248,14 +265,23 @@
 
     lax.fori_loop(0, D_MODEL // 128, turn, 0)
 
-    wait(given_v.at[: ((ROWS - HALF) + (HALF - BLOCK) + 2 * HALF) // 2], last_r)
-
-    def end(rows):
-        blocks = 2 * (ROWS - BLOCK) + 2 * HALF + 2 * (BLOCK + rows)
-        sums_and_router = 3 * BLOCKS // 2 + 3 * 2 + 3 * 8 + 7 * 32 + 256
-        wait(given_v.at[: (blocks + sums_and_router) // 2], out_sem)
-
-    by_core(end)
+    def end(shift):
+        wait(given_v.at[: (2 * ROWS - BLOCK + shift) // 2], last_r)
+
+        def end_core(rows):
+            blocks = 2 * (ROWS - BLOCK) + ROWS - shift + 2 * (BLOCK + rows)
+            sums_and_router = 3 * BLOCKS // 2 + 3 * 2 + 3 * 8 + 7 * 32 + 256
+            wait(given_v.at[: (blocks + sums_and_router) // 2], out_sem)
+
+        by_core(end_core)
+
+    @pl.when((me == 0) | (me == 3))
+    def _():
+        end(SHIFT)
+
+    @pl.when((me == 1) | (me == 2))
+    def _():
+        end(-SHIFT)
 
 
 def write(ready, scale, router, latest, ready_out, scale_out, router_out, latest_out, sem):

time: 62.1 us -> 61.8 us (level)
  no operation moved by 1% of the time
where the time goes in v5:
time: 61.8 us; the launch traced here: 61.7 us
  Pallas kernels  61.1 us (99%)
  between operations  0.64 us (1%)
    pallas_call x1, Pallas kernels, shards(): pl.pallas_call(kernel, out_shape=tuple((pltpu.VMEM(*k) for k in shapes)),...  57.3 us
    pallas_call x1, Pallas kernels, shards(): pl.pallas_call(write, out_shape=tuple((pltpu.HBM(*k) for k in shapes)), i...  3.85 us

profile of v5, /device:TPU:8, one launch (start us, length us, event | category | flops | bytes accessed | tf_op | source)
XLA Modules:
  0.0 61.7 jit_solution(10416817826924926443)
XLA Ops:
  0.6 57.3 %shard_map.75 = (bf16[1536,2048]{1,0:T(8,128)(2,1)S(1)}, f32[2,768]{1,0:T(2,128)S(1)}, bf16[2048,128]{1,0:T(8,128)(2,1)S(1)}, f32[1536,512]{1,0:T(8,128)S(1)}) custom-call(f32[1536,512]{1,0:T(8,128)} %bitcast.6, f32[1536,512]{1,0:T(8,128)} %bitcast.7, f32[2,512]{1,0:T(2,128)} %bitcast.8, f32[1,512]{1,0:T(1,128)} %bitcast.9), custom_call_target="tpu_custom_call" | custom-call | tf_op jit(solution)/shard_map/pallas_call | solution.py:306
  57.9 3.8 %shard_map.76 = (bf16[1536,2048]{1,0:T(8,128)(2,1)}, f32[2,768]{1,0:T(2,128)}, bf16[2048,128]{1,0:T(8,128)(2,1)}, f32[1536,512]{1,0:T(8,128)}) custom-call(bf16[1536,2048]{1,0:T(8,128)(2,1)S(1)} %get-tuple-element.12.ready, f32[2,768]{1,0:T(2,128)S(1)} %get-tuple-element.13.scale, bf16[2048,128]{1,0:T(8,128)(2,1)S(1)} %get-tuple-element.14.router, ...), custom_call_target="tpu_custom_call" | custom-call | tf_op jit(solution)/shard_map/pallas_call | solution.py:326

commit v6 on v5

--- a/solution.py
+++ b/solution.py
@@ -157,9 +157,9 @@
         narrow_fill(1, left, rows)
 
     average(0)
+    average(1)
     for c in range(2, len(READS) - 1):
         start_read(c)
-    average(1)
     for copy in small:
         copy.wait()
     rows_r[z, y, core, me] = (weight_v[...] * gain_v[...]).astype(jnp.bfloat16)

time: 61.8 us -> 61.8 us (level)
  no operation moved by 1% of the time
where the time goes in v6:
time: 61.8 us; the launch traced here: 61.7 us
  Pallas kernels  61.1 us (99%)
  between operations  0.64 us (1%)
    pallas_call x1, Pallas kernels, shards(): pl.pallas_call(kernel, out_shape=tuple((pltpu.VMEM(*k) for k in shapes)),...  57.3 us
    pallas_call x1, Pallas kernels, shards(): pl.pallas_call(write, out_shape=tuple((pltpu.HBM(*k) for k in shapes)), i...  3.85 us

profile of v6, /device:TPU:8, one launch (start us, length us, event | category | flops | bytes accessed | tf_op | source)
XLA Modules:
  0.0 61.7 jit_solution(9879772140648661023)
XLA Ops:
  0.6 57.3 %shard_map.75 = (bf16[1536,2048]{1,0:T(8,128)(2,1)S(1)}, f32[2,768]{1,0:T(2,128)S(1)}, bf16[2048,128]{1,0:T(8,128)(2,1)S(1)}, f32[1536,512]{1,0:T(8,128)S(1)}) custom-call(f32[1536,512]{1,0:T(8,128)} %bitcast.6, f32[1536,512]{1,0:T(8,128)} %bitcast.7, f32[2,512]{1,0:T(2,128)} %bitcast.8, f32[1,512]{1,0:T(1,128)} %bitcast.9), custom_call_target="tpu_custom_call" | custom-call | tf_op jit(solution)/shard_map/pallas_call | solution.py:306
  57.9 3.8 %shard_map.76 = (bf16[1536,2048]{1,0:T(8,128)(2,1)}, f32[2,768]{1,0:T(2,128)}, bf16[2048,128]{1,0:T(8,128)(2,1)}, f32[1536,512]{1,0:T(8,128)}) custom-call(bf16[1536,2048]{1,0:T(8,128)(2,1)S(1)} %get-tuple-element.12.ready, f32[2,768]{1,0:T(2,128)S(1)} %get-tuple-element.13.scale, bf16[2048,128]{1,0:T(8,128)(2,1)S(1)} %get-tuple-element.14.router, ...), custom_call_target="tpu_custom_call" | custom-call | tf_op jit(solution)/shard_map/pallas_call | solution.py:326

commit v7 on v6

--- a/solution.py
+++ b/solution.py
@@ -12,8 +12,8 @@
 BLOCK = 128
 BLOCKS = ROWS // BLOCK
 FILL = (48, 64)
-READS = (0, 128, 256, 768, 1536)
-EARLY = 256
+READS = (0, 128, 384, 768, 1536)
+EARLY = 384
 HALF = ROWS // 2
 SHIFT = 32
 NZ, NY, NC, NX = 8, 4, 2, 4

time: 61.8 us -> 61.9 us (level)
  no operation moved by 1% of the time
where the time goes in v7:
time: 61.9 us; the launch traced here: 61.8 us
  Pallas kernels  61.2 us (99%)
  between operations  0.64 us (1%)
    pallas_call x1, Pallas kernels, shards(): pl.pallas_call(kernel, out_shape=tuple((pltpu.VMEM(*k) for k in shapes)),...  57.3 us
    pallas_call x1, Pallas kernels, shards(): pl.pallas_call(write, out_shape=tuple((pltpu.HBM(*k) for k in shapes)), i...  3.85 us

profile of v7, /device:TPU:8, one launch (start us, length us, event | category | flops | bytes accessed | tf_op | source)
XLA Modules:
  0.0 61.8 jit_solution(7878178697705972345)
XLA Ops:
  0.6 57.3 %shard_map.75 = (bf16[1536,2048]{1,0:T(8,128)(2,1)S(1)}, f32[2,768]{1,0:T(2,128)S(1)}, bf16[2048,128]{1,0:T(8,128)(2,1)S(1)}, f32[1536,512]{1,0:T(8,128)S(1)}) custom-call(f32[1536,512]{1,0:T(8,128)} %bitcast.6, f32[1536,512]{1,0:T(8,128)} %bitcast.7, f32[2,512]{1,0:T(2,128)} %bitcast.8, f32[1,512]{1,0:T(1,128)} %bitcast.9), custom_call_target="tpu_custom_call" | custom-call | tf_op jit(solution)/shard_map/pallas_call | solution.py:306
  58.0 3.8 %shard_map.76 = (bf16[1536,2048]{1,0:T(8,128)(2,1)}, f32[2,768]{1,0:T(2,128)}, bf16[2048,128]{1,0:T(8,128)(2,1)}, f32[1536,512]{1,0:T(8,128)}) custom-call(bf16[1536,2048]{1,0:T(8,128)(2,1)S(1)} %get-tuple-element.12.ready, f32[2,768]{1,0:T(2,128)S(1)} %get-tuple-element.13.scale, bf16[2048,128]{1,0:T(8,128)(2,1)S(1)} %get-tuple-element.14.router, ...), custom_call_target="tpu_custom_call" | custom-call | tf_op jit(solution)/shard_map/pallas_call | solution.py:326
